TPU v7x, 32 devices: a whole 2x2x4 slice. The times are simulated.
32 devices in a mesh: row: 4 (over x, core), col: 8 (over z, y).
Axes of the slice: x: 2, y: 2, z: 4, core: 2. Of those that a mesh axis runs over, the one named last changes fastest.
Arguments:
- hamiltonian: bfloat16 [2912, 2912], P('row', 'col'), may hold values from -6 to 6
- new_atom: int32 [224], replicated, may hold values from 0 to 223, as said below
- pattern: int32 [224, 224], P('row', 'col'), may hold values 0 or 1
Outputs:
- sign_matrix: float32 [2912, 2912], P('row', 'col')
Inputs may be any that keep to these rules, and one draw needn't show every extreme that they name: `new_atom`: each old atom appears once. Block column b holds atoms b * 28 to (b + 1) * 28 - 1 in both orders. For each new block column d and each v from 0 to 27, exactly one atom of new block column d comes from old block column (d - 1 - (v mod 8)) mod 8, so the number of atoms that old block column b sends to new block column (b + k) mod 8 is the number of such v with (1 + v) mod 8 = k.
All inputs are finite; a program needn't handle non-finite values. No bound on the sum of `pattern` on one device may be relied on, other than what follows from the above.
Results may differ from a plain program's by a relative error of at most 0.0029.
Values may be sent and summed in bfloat16 or wider, within the bound.
A program may use at most 64 MiB of HBM per device.

v0:
```python
import jax
import jax.numpy as jnp
import numpy as np
from jax import lax
from jax.sharding import PartitionSpec as P

NBF = 13


def expand(atoms):
    return (atoms[:, None] * NBF + jnp.arange(NBF, dtype=jnp.int32)[None, :]).reshape(-1)


def pack_slots(new_atom, here, per_block, groups, slots):
    source = new_atom.reshape(groups, per_block) // per_block
    local = new_atom.reshape(groups, per_block) - here * per_block
    mine = source == here
    rank = jnp.cumsum(mine.astype(jnp.int32), axis=1) - 1
    number = jnp.arange(slots, dtype=jnp.int32)
    hit = mine[:, None, :] & (rank[:, None, :] == number[None, :, None])
    atoms = jnp.sum(jnp.where(hit, local[:, None, :], 0), axis=2)
    used = jnp.any(hit, axis=2)
    return (atoms.reshape(-1), jnp.repeat(used.reshape(-1), NBF))


def place_slots(new_atom, here, per_block, groups, slots):
    source = lax.dynamic_slice_in_dim(new_atom, here * per_block, per_block) // per_block
    onehot = source[:, None] == jnp.arange(groups, dtype=jnp.int32)[None, :]
    running = jnp.cumsum(onehot.astype(jnp.int32), axis=0) - 1
    rank = jnp.sum(jnp.where(onehot, running, 0), axis=1)
    return expand((source * slots + rank).astype(jnp.int32))


def fold_right(row_panel, right):
    return jnp.dot(
        row_panel,
        lax.all_gather(right, "row", axis=0, tiled=True),
        preferred_element_type=jnp.float32,
    )


def on_device(hamiltonian, new_atom, pattern):
    rows_here, cols_here = hamiltonian.shape
    row_count = lax.axis_size("row")
    col_count = lax.axis_size("col")
    order_all = rows_here * row_count
    atoms_row = rows_here // NBF
    atoms_col = cols_here // NBF
    ratio = col_count // row_count
    counts = np.bincount((1 + np.arange(atoms_col)) % col_count, minlength=col_count)
    targets = (np.arange(ratio)[:, None] + np.arange(col_count)[None, :]) % col_count // ratio
    per_target = np.sum(
        (targets[None, :, :] == np.arange(row_count)[:, None, None]) * counts[None, None, :],
        axis=(1, 2),
    )
    slots_row = max(int(np.max(per_target)), 1)
    slots_col = max(int(np.max(counts)), 1)
    row_here = lax.axis_index("row")
    col_here = lax.axis_index("col")
    atoms, flags = pack_slots(new_atom, row_here, atoms_row, row_count, slots_row)
    outgoing = jnp.where(
        flags[:, None], jnp.take(hamiltonian, expand(atoms), axis=0), jnp.zeros((), jnp.bfloat16)
    )
    arrived = lax.all_to_all(outgoing, "row", split_axis=0, concat_axis=0, tiled=True)
    moved = jnp.take(
        arrived, place_slots(new_atom, row_here, atoms_row, row_count, slots_row), axis=0
    )
    atoms, flags = pack_slots(new_atom, col_here, atoms_col, col_count, slots_col)
    outgoing = jnp.where(
        flags[None, :], jnp.take(moved, expand(atoms), axis=1), jnp.zeros((), jnp.bfloat16)
    )
    arrived = lax.all_to_all(outgoing, "col", split_axis=1, concat_axis=1, tiled=True)
    moved = jnp.take(
        arrived, place_slots(new_atom, col_here, atoms_col, col_count, slots_col), axis=1
    )
    atom_rows, atom_cols = pattern.shape
    keep = jnp.broadcast_to(
        pattern.astype(jnp.float32)[:, None, :, None], (atom_rows, NBF, atom_cols, NBF)
    ).reshape(rows_here, cols_here)
    masked = moved.astype(jnp.float32) * keep
    total = lax.psum(jnp.sum(masked * masked), ("row", "col"))
    start = (masked * lax.rsqrt(total / order_all)).astype(jnp.bfloat16)
    first = lax.all_gather(start, "col", axis=1, tiled=True)
    square = (fold_right(first, start) * keep).astype(jnp.bfloat16)
    second = lax.all_gather(start, "col", axis=1, tiled=True)
    cube = fold_right(second, square) * keep
    return keep * (1.5 * start.astype(jnp.float32) - 0.5 * cube)


def solution(mesh):
    in_specs = (P("row", "col"), P(), P("row", "col"))
    out_specs = P("row", "col")
    return jax.shard_map(
        on_device, mesh=mesh, in_specs=in_specs, out_specs=out_specs, check_vma=False
    )
```

profile of v0, /device:TPU:0, one launch (start us, length us, event | category | flops | bytes accessed | tf_op | source)
XLA Modules:
  0.0 246.0 jit_solution(5118682109715307969)
XLA Ops:
  6.5 0.8 compare_and_fusion.5
  7.3 0.7 broadcast_divide_fusion.1
  8.3 0.2 reduce_window_sum.47
  8.5 0.2 fusion.9
  8.6 0.2 select_reduce_fusion
  9.0 0.2 add.307
  9.5 0.1 broadcast_in_dim.144
  9.6 3.5 %gather_fusion = bf16[832,364]{1,0:T(8,128)(2,1)S(1)} fusion(bf16[728,364]{1,0:T(8,128)(2,1)S(1)} %copy-done, s32[1024]{0:T(1024)S(1)} %pad_clamp_fusion.3), kind=kCustom, calls=%fused_computation | custom fusion | bytes 1214720 | tf_op jit(solution)/shard_map/jit(_take)/gather | solution.py:62
  13.2 1.1 select_select_fusion.1
  14.3 4.2 %all-to-all-start = ((bf16[4,208,364]{2,1,0:T(8,128)(2,1)}), bf16[4,208,364]{2,1,0:T(8,128)(2,1)S(1)}, u32[]{:S(2)}, u32[]{:S(2)}) async-start(bf16[4,208,364]{2,1,0:T(8,128)(2,1)} %select_select_fusion.1), calls=%async_computation | async-start | bytes 1277952 | tf_op jit(solution)/shard_map/all_to_all | solution.py:64
  18.8 0.2 select_reduce_fusion.1
  19.1 0.1 add.310
  19.6 0.2 reduce_window_sum.45
  19.8 0.1 fusion.13
  19.9 0.2 select_reduce_fusion.2
  20.3 0.1 add.316
  20.5 0.1 add.294
  21.2 7.4 %all-to-all-done = bf16[4,208,364]{2,1,0:T(8,128)(2,1)S(1)} async-done(((bf16[4,208,364]{2,1,0:T(8,128)(2,1)}), bf16[4,208,364]{2,1,0:T(8,128)(2,1)S(1)}, u32[]{:S(2)}, u32[]{:S(2)}) %all-to-all-start) | async-done | bytes 605728 | tf_op jit(solution)/shard_map/all_to_all | solution.py:64
  28.6 3.0 %gather_fusion.1 = bf16[728,364]{1,0:T(8,128)(2,1)S(1)} fusion(bf16[832,364]{1,0:T(8,128)(2,1)S(1)} %bitcast.33, s32[1024]{0:T(1024)S(1)} %pad_clamp_fusion.2), kind=kCustom, calls=%fused_computation.1 | custom fusion | bytes 1062880 | tf_op jit(solution)/shard_map/jit(_take)/gather | solution.py:65
  31.5 0.2 broadcast_select_fusion
  31.7 0.2 copy.28
  32.0 2.2 gather_fusion.2
  34.1 0.1 gather.24
  34.3 1.0 select_select_fusion
  35.3 6.5 %all-to-all-start.1 = ((bf16[728,8,52]{0,2,1:T(8,128)(2,1)}), bf16[728,8,52]{0,2,1:T(8,128)(2,1)S(1)}, u32[]{:S(2)}, u32[]{:S(2)}) async-start(bf16[728,8,52]{0,2,1:T(8,128)(2,1)} %select_select_fusion), calls=%async_computation.1 | async-start | bytes 1376256 | tf_op jit(solution)/shard_map/all_to_all | solution.py:72
  42.0 0.2 select_reduce_fusion.3
  42.4 0.1 add.319
  42.5 0.1 add.279
  42.6 4.7 %broadcast_in_dim.132 = f32[56,13,28,13]{1,0,3,2:T(8,128)} broadcast(f32[56,28]{0,1:T(8,128)S(1)} %convert_element_type.41), dimensions={0,2} | broadcast | bytes 1066240 | tf_op jit(solution)/shard_map/broadcast_in_dim | solution.py:77
  47.3 6.7 %reshape.368 = f32[728,364]{0,1:T(8,128)S(1)} reshape(f32[56,13,28,13]{1,0,3,2:T(8,128)} %broadcast_in_dim.132) | data formatting | bytes 2119936 | tf_op jit(solution)/shard_map/reshape | solution.py:79
  54.1 0.4 copy.36
  54.5 0.1 broadcast_in_dim.154
  54.7 4.9 %all-to-all-done.1 = bf16[728,8,52]{0,2,1:T(8,128)(2,1)S(1)} async-done(((bf16[728,8,52]{0,2,1:T(8,128)(2,1)}), bf16[728,8,52]{0,2,1:T(8,128)(2,1)S(1)}, u32[]{:S(2)}, u32[]{:S(2)}) %all-to-all-start.1) | async-done | bytes 605728 | tf_op jit(solution)/shard_map/all_to_all | solution.py:72
  59.6 0.3 all_to_all.15
  59.8 2.2 gather_fusion.3
  62.0 0.3 copy.29
  62.3 0.9 fusion.5
  63.2 38.4 %psum.7 = f32[]{:T(128)} all-reduce(f32[]{:T(128)} %fusion.5), channel_id=1, replica_groups=mesh['row'=4,'col'=8] {'row','col'}, use_global_device_ids=true, to_apply=%region_11.12 | all-reduce | flops 1 | bytes 8 | tf_op jit(solution)/shard_map/psum | solution.py:81
  102.3 1.0 fusion.7
  103.3 0.7 all-gather.5.cloned.1.call-update
  104.1 0.2 all-gather.7.cloned.1.call-start
  104.3 75.6 %all-gather.9.cloned.1.call-done = bf16[8,364,728]{1,2,0:T(8,128)(2,1)} async-done(((bf16[1,364,728]{1,2,0:T(8,128)(2,1)}), bf16[8,364,728]{1,2,0:T(8,128)(2,1)}) %all-gather.9.cloned.1.call-update) | async-done | bytes 4239888 | tf_op jit(solution)/shard_map/all_gather | solution.py:85
  179.9 4.9 %copy.33 = bf16[8,364,728]{1,0,2:T(8,128)(2,1)} copy(bf16[8,364,728]{1,2,0:T(8,128)(2,1)} %all-gather.9.cloned.1.call-done) | data formatting | bytes 8479744 | tf_op jit(solution)/shard_map/all_gather | solution.py:85
  184.8 8.7 %reshape.402 = bf16[2912,728]{0,1:T(8,128)(2,1)} reshape(bf16[8,364,728]{1,0,2:T(8,128)(2,1)} %copy.33) | data formatting | bytes 8479744
  193.5 9.8 %all-gather.5.cloned.1.call-done = bf16[2912,364]{1,0:T(8,128)(2,1)} async-done(((bf16[728,364]{1,0:T(8,128)(2,1)}), bf16[2912,364]{1,0:T(8,128)(2,1)}) %all-gather.5.cloned.1.call-update) | async-done | bytes 2119952 | tf_op jit(solution)/shard_map/all_gather | solution.py:37
  203.3 6.2 %fusion.3 = bf16[728,364]{1,0:T(8,128)(2,1)} fusion(f32[728,364]{1,0:T(8,128)S(1)} %copy.36, bf16[2912,728]{0,1:T(8,128)(2,1)} %reshape.402, bf16[2912,364]{1,0:T(8,128)(2,1)} %all-gather.5.cloned.1.call-done), kind=kOutput, calls=%fused_computation.9 | convolution fusion | flops 1543843328 | bytes 7949760 | tf_op jit(solution)/shard_map/dot_general | solution.py:35
  209.5 23.5 %all-gather.7.cloned.1.call-done = bf16[2912,364]{1,0:T(8,128)(2,1)} async-done(((bf16[728,364]{1,0:T(8,128)(2,1)}), bf16[2912,364]{1,0:T(8,128)(2,1)}) %all-gather.7.cloned.1.call-update) | async-done | bytes 2119952 | tf_op jit(solution)/shard_map/all_gather | solution.py:37
  233.0 6.4 %fusion.2 = f32[728,364]{1,0:T(8,128)} fusion(f32[728,364]{1,0:T(8,128)S(1)} %copy.36, bf16[2912,728]{0,1:T(8,128)(2,1)} %reshape.402, bf16[2912,364]{1,0:T(8,128)(2,1)} %all-gather.7.cloned.1.call-done, bf16[728,364]{1,0:T(8,128)(2,1)S(1)} %copy-done.1), kind=kOutput, calls=%fused_computation.8 | convolution fusion | flops 1544903168 | bytes 9009728 | tf_op jit(solution)/shard_map/dot_general | solution.py:35
  (65 shorter events, 2.9 us)
Async XLA Ops:
  6.5 3.1 %copy-start = (bf16[728,364]{1,0:T(8,128)(2,1)S(1)}, bf16[728,364]{1,0:T(8,128)(2,1)}, u32[]{:S(2)}) copy-start(bf16[728,364]{1,0:T(8,128)(2,1)} %param.3) | copy-start | bytes 1589956
  13.1 5.4 %copy-start.3 = (s32[224]{0:T(256)S(1)}, s32[224]{0:T(256)}, u32[]{:S(2)}) copy-start(s32[224]{0:T(256)} %param.4) | copy-start | bytes 2692
  14.3 14.3 %all-to-all-start = ((bf16[4,208,364]{2,1,0:T(8,128)(2,1)}), bf16[4,208,364]{2,1,0:T(8,128)(2,1)S(1)}, u32[]{:S(2)}, u32[]{:S(2)}) async-start(bf16[4,208,364]{2,1,0:T(8,128)(2,1)} %select_select_fusion.1), calls=%async_computation | async-start | bytes 1277952 | tf_op jit(solution)/shard_map/all_to_all | solution.py:64
  34.3 8.3 %copy-start.2 = (s32[56,28]{0,1:T(8,128)S(1)}, s32[56,28]{0,1:T(8,128)}, u32[]{:S(2)}) copy-start(s32[56,28]{0,1:T(8,128)} %param.5) | copy-start | bytes 18820
  35.3 24.2 %all-to-all-start.1 = ((bf16[728,8,52]{0,2,1:T(8,128)(2,1)}), bf16[728,8,52]{0,2,1:T(8,128)(2,1)S(1)}, u32[]{:S(2)}, u32[]{:S(2)}) async-start(bf16[728,8,52]{0,2,1:T(8,128)(2,1)} %select_select_fusion), calls=%async_computation.1 | async-start | bytes 1376256 | tf_op jit(solution)/shard_map/all_to_all | solution.py:72
  41.9 138.0 %all-gather.9.cloned.1.call-start = ((), (), s32[]{:S(2)}) async-start(), calls=%async_computation.4 | async-start | bytes 5031936 | tf_op jit(solution)/shard_map/all_gather | solution.py:85
  103.3 100.0 %all-gather.5.cloned.1.call-start = ((), (), s32[]{:S(2)}) async-start(), calls=%async_computation.2 | async-start | bytes 2795520 | tf_op jit(solution)/shard_map/all_gather | solution.py:37
  104.1 129.0 %all-gather.7.cloned.1.call-start = ((), (), s32[]{:S(2)}) async-start(), calls=%async_computation.3 | async-start | bytes 2795520 | tf_op jit(solution)/shard_map/all_gather | solution.py:37
  193.5 39.5 %copy-start.1 = (bf16[728,364]{1,0:T(8,128)(2,1)S(1)}, bf16[728,364]{1,0:T(8,128)(2,1)}, u32[]{:S(2)}) copy-start(bf16[728,364]{1,0:T(8,128)(2,1)} %fusion.7) | copy-start | bytes 1589956
Sparse Core Ops, SparseCore 0:
  103.4 76.4 all-gather.8
  181.4 21.7 all-gather.4
  209.7 23.3 all-gather.6
where the time goes:
time: 247 us; the launch traced here: 246 us
  waiting for transfers between devices  122 us (49%)
  local copies, waits for them, and re-layouts  39.7 us (16%)
  blocking collectives  38.4 us (16%)
  between operations  14.1 us (6%)
  matrix products  12.7 us (5%)
  starting transfers between devices  11.1 us (4%)
  other arithmetic  8.25 us (3%)
    all_gather x1, waiting for transfers between devices, on_device(): second = lax.all_gather(start, 'col', axis=1, tiled=True)  75.6 us
    psum x1, blocking collectives, on_device(): total = lax.psum(jnp.sum(masked * masked), ('row', 'col'))  38.4 us
    all_gather x2, waiting for transfers between devices, fold_right(): lax.all_gather(right, 'row', axis=0, tiled=True)  33.3 us
    dot_general x2, matrix products, fold_right(): jnp.dot(row_panel, lax.all_gather(right, 'row', axis=0, tiled=True), pref...  12.7 us
    unnamed x9, local copies, waits for them, and re-layouts  8.69 us
    all_to_all x1, waiting for transfers between devices, on_device(): lax.all_to_all(outgoing, 'row', split_axis=0, concat_axis=0, tiled=True)  7.35 us
    reshape x2, local copies, waits for them, and re-layouts, on_device(): keep = jnp.broadcast_to(pattern.astype(jnp.float32)[:, None, :, None], (a...  7.1 us
    all_to_all x1, starting transfers between devices, on_device(): lax.all_to_all(outgoing, 'col', split_axis=1, concat_axis=1, tiled=True)  6.53 us
  transfers between devices with their start and end apart: 5, of which 5 were waited for; matrix products, arithmetic and copies ran while one was open for 12% of the time, Pallas kernels for 0%

commit v1 on v0

v1 whole, which is shorter than its diff:
```python
import jax
import jax.numpy as jnp
from jax import lax
from jax.sharding import PartitionSpec as P

NBF = 13
BF = jnp.bfloat16
F32 = jnp.float32


def mm(a, b):
    return jnp.dot(a, b, preferred_element_type=F32)


def spread(n):
    i = lax.broadcasted_iota(jnp.int32, (n * NBF, n), 0)
    a = lax.broadcasted_iota(jnp.int32, (n * NBF, n), 1) * NBF
    return (i >= a) & (i < a + NBF)


def on_device(hamiltonian, new_atom, pattern):
    rows_here, cols_here = hamiltonian.shape
    order = rows_here * lax.axis_size("row")
    atoms = order // NBF
    ar, ac = pattern.shape
    row_here = lax.axis_index("row")
    col_here = lax.axis_index("col")
    panel = lax.all_gather(hamiltonian, "col", axis=1, tiled=True)
    pat = lax.all_gather(pattern.astype(BF), ("row", "col"), axis=0, tiled=False)
    n_row, n_col = lax.axis_size("row"), lax.axis_size("col")
    pat = pat.reshape(n_row, n_col, ar, ac).transpose(0, 2, 1, 3).reshape(atoms, atoms)
    old = jnp.arange(atoms, dtype=jnp.int32)
    perm = (new_atom[:, None] == old[None, :]).astype(BF)
    mine = (new_atom[None, :] == row_here * ar + jnp.arange(ar, dtype=jnp.int32)[:, None]).astype(BF)
    pat_rows = mm(mine, pat).astype(BF)
    e_row = spread(ar)
    e_col = spread(ac)
    e_rowb = e_row.astype(BF)
    rows_masked = mm(e_rowb, mm(pat_rows, perm).astype(BF)).astype(BF)
    keep = mm(rows_masked, spread(atoms).astype(BF).T).astype(BF)
    m = panel * keep
    total = lax.psum(jnp.sum(m.astype(F32) ** 2), "row")
    s = lax.rsqrt(total / order)

    def old_index(n, here, e):
        mine_atoms = lax.dynamic_slice_in_dim(new_atom, here * n, n)
        base = jnp.sum(jnp.where(e, (mine_atoms - jnp.arange(n, dtype=jnp.int32))[None, :], 0), axis=1)
        return base * NBF + jnp.arange(n * NBF, dtype=jnp.int32)

    full = jnp.arange(order, dtype=jnp.int32)
    pick_col = (full[:, None] == old_index(ac, col_here, e_col)[None, :]).astype(BF)
    pick_row = (old_index(ar, row_here, e_row)[:, None] == full[None, :]).astype(BF)
    right = lax.all_gather(mm(m, pick_col).astype(BF), "row", axis=0, tiled=True)
    e_colt = e_col.astype(BF).T
    here_cols = lax.dynamic_slice_in_dim(pat_rows, col_here * ac, ac, axis=1)
    keep_sq = mm(mm(e_rowb, here_cols).astype(BF), e_colt)
    square = (mm(m, right) * (s * s) * keep_sq).astype(BF)
    square = lax.all_gather(square, "row", axis=0, tiled=True)
    cube = lax.all_gather((mm(m, square) * s).astype(BF), "row", axis=0, tiled=True)
    start = (mm(pick_row, right) * s).astype(BF).astype(F32)
    keep_out = mm(mm(e_rowb, pattern.astype(BF)).astype(BF), e_colt)
    return keep_out * (1.5 * start - 0.5 * mm(pick_row, cube))


def solution(mesh):
    in_specs = (P("row", "col"), P(), P("row", "col"))
    out_specs = P("row", "col")
    return jax.shard_map(
        on_device, mesh=mesh, in_specs=in_specs, out_specs=out_specs, check_vma=False
    )
```

time: 247 us -> 212 us (0.86)
  waiting for transfers between devices: 122 us -> 64.9 us
  blocking collectives: 38.4 us -> 81.4 us
  local copies, waits for them, and re-layouts: 39.7 us -> 13.8 us
  matrix products: 12.7 us -> 35.5 us
  starting transfers between devices: 11.1 us -> 0.31 us
  other arithmetic: 8.25 us -> 1.79 us
    all_gather x0 -> x1, blocking collectives: none -> 75.1 us  [on_device(): lax.all_gather(pattern.astype(BF), ('row', 'col'), axis=0, tiled=False)]
    all_gather x3 -> x4, waiting for transfers between devices: 109 us -> 64.2 us  [the longest x1 23.3 us: on_device(): square = lax.all_gather(square, 'row', axis=0, tiled=True)]
    psum x1, blocking collectives: 38.4 us -> 6.25 us  [on_device(): total = lax.psum(jnp.sum(m.astype(F32) ** 2), 'row')]
    dot_general x2 -> x10, matrix products: 12.7 us -> 35.5 us  [mm(): return jnp.dot(a, b, preferred_element_type=F32)]
    all_to_all x2 -> x0, waiting for transfers between devices: 12.3 us -> none  [the longest x1 7.35 us: on_device(): lax.all_to_all(outgoing, 'row', split_axis=0, concat_axis=0, tiled=True)]
    gather x6 -> x0, local copies, waits for them, and re-layouts: 11.2 us -> none  [the longest x1 3.49 us: on_device(): jnp.take(hamiltonian, expand(atoms), axis=0)]
    all_to_all x2 -> x0, starting transfers between devices: 10.8 us -> none  [the longest x1 6.53 us: on_device(): lax.all_to_all(outgoing, 'col', split_axis=1, concat_axis=1, tiled=True)]
    reshape x2, local copies, waits for them, and re-layouts: 7.1 us -> 0.35 us  [on_device(): pat.reshape(n_row, n_col, ar, ac).transpose(0, 2, 1, 3)]
  transfers between devices with their start and end apart: 5 -> 4, of which waited for: 5 -> 4; matrix products, arithmetic and copies ran while one was open for 12% -> 3% of each run, Pallas kernels for 0% -> 0%
where the time goes in v1:
time: 212 us
  blocking collectives  81.4 us (38%)
  waiting for transfers between devices  64.9 us (31%)
  matrix products  35.5 us (17%)
  between operations  14 us (7%)
  local copies, waits for them, and re-layouts  13.8 us (7%)
    all_gather x1, blocking collectives, on_device(): lax.all_gather(pattern.astype(BF), ('row', 'col'), axis=0, tiled=False)  75.1 us
    dot_general x10, matrix products, mm(): return jnp.dot(a, b, preferred_element_type=F32)  35.5 us
    all_gather x1, waiting for transfers between devices, on_device(): square = lax.all_gather(square, 'row', axis=0, tiled=True)  23.3 us
    all_gather x1, waiting for transfers between devices, on_device(): lax.all_gather((mm(m, square) * s).astype(BF), 'row', axis=0, tiled=True)  20.7 us
    all_gather x1, waiting for transfers between devices, on_device(): lax.all_gather(mm(m, pick_col).astype(BF), 'row', axis=0, tiled=True)  15.2 us
    unnamed x7, local copies, waits for them, and re-layouts  8.62 us
    psum x1, blocking collectives, on_device(): total = lax.psum(jnp.sum(m.astype(F32) ** 2), 'row')  6.25 us
    all_gather x1, waiting for transfers between devices, on_device(): panel = lax.all_gather(hamiltonian, 'col', axis=1, tiled=True)  5 us
  transfers between devices with their start and end apart: 4, of which 4 were waited for; matrix products, arithmetic and copies ran while one was open for 3% of the time, Pallas kernels for 0%

profile of v1, /device:TPU:0, one launch (start us, length us, event | category | flops | bytes accessed | tf_op | source)
XLA Modules:
  0.0 211.8 jit_solution(7994260219636314159)
XLA Ops:
  6.5 0.0 all-gather.14.cloned.1.call-start
  6.5 0.7 all-gather.14.cloned.1.call-update
  7.3 0.0 all-gather.8.cloned.1.call-start
  7.3 0.7 convert_bitcast_fusion
  8.0 75.1 %all-gather.2 = bf16[32,56,28]{1,2,0:T(8,128)(2,1)S(1)} all-gather(bf16[1,56,28]{1,2,0:T(8,128)(2,1)S(1)} %convert_bitcast_fusion), channel_id=2, replica_groups=mesh['row'=4,'col'=8] {'row','col'}, dimensions={0}, use_global_device_ids=true | all-gather | bytes 103488 | tf_op jit(solution)/shard_map/all_gather | solution.py:29
  83.2 0.2 copy.12
  83.3 0.2 reshape.30
  83.5 0.8 iota_subtract_fusion
  84.3 0.1 select_reduce_fusion.1
  84.4 0.9 convolution_convert_fusion.5
  85.3 0.9 convolution_convert_fusion.4
  86.2 5.0 %all-gather.14.cloned.1.call-done = bf16[8,364,728]{1,2,0:T(8,128)(2,1)} async-done(((bf16[1,364,728]{1,2,0:T(8,128)(2,1)}), bf16[8,364,728]{1,2,0:T(8,128)(2,1)}) %all-gather.14.cloned.1.call-update) | async-done | bytes 4239888 | tf_op jit(solution)/shard_map/all_gather | solution.py:28
  91.2 4.9 %copy.9 = bf16[8,364,728]{1,0,2:T(8,128)(2,1)} copy(bf16[8,364,728]{1,2,0:T(8,128)(2,1)} %all-gather.14.cloned.1.call-done) | data formatting | bytes 8479744 | tf_op jit(solution)/shard_map/all_gather | solution.py:28
  96.1 8.6 %reshape.34 = bf16[2912,728]{0,1:T(8,128)(2,1)} reshape(bf16[8,364,728]{1,0,2:T(8,128)(2,1)} %copy.9) | data formatting | bytes 8479744
  104.7 6.9 %multiply_reduce_fusion = (f32[]{:T(128)}, bf16[728,2912]{1,0:T(8,128)(2,1)}) fusion(s32[224]{0:T(256)S(1)} %get-tuple-element.8, s32[224]{0:T(256)S(1)} %get-tuple-element.7, bf16[56,224]{1,0:T(8,128)(2,1)S(1)} %convolution_convert_fusion.4, s32[56]{0:T(128)S(1)} %get-tuple-element.10, s32[56]{0:T(128)S(1)} %get-tuple-element.9, bf16[2912,728]{0,1:T(8,128)(2,1)} %reshape.34), kind=kOutput, calls=%fused_computation | convolution fusion | flops 987197120 | bytes 8507076 | tf_op jit(solution)/shard_map/dot_general | solution.py:12
  111.6 5.5 %fusion.19 = bf16[728,364]{1,0:T(8,128)(2,1)} fusion(bf16[728,2912]{1,0:T(8,128)(2,1)} %get-tuple-element.6, s32[364]{0:T(512)S(1)} %iota_add_fusion.1), kind=kOutput, calls=%fused_computation.28 | convolution fusion | flops 1544638336 | bytes 4771312 | tf_op jit(solution)/shard_map/dot_general | solution.py:12
  117.1 0.0 all-gather.8.cloned.1.call-update
  117.1 0.0 all-gather.10.cloned.1.call-start
  117.2 6.2 %psum.7 = f32[]{:T(128)} all-reduce(f32[]{:T(128)} %get-tuple-element.5), channel_id=1, replica_groups=mesh['row'=4,'col'=8] {'row'}, use_global_device_ids=true, to_apply=%region_3.4 | all-reduce | flops 1 | bytes 8 | tf_op jit(solution)/shard_map/psum | solution.py:42
  124.2 15.2 %all-gather.8.cloned.1.call-done = bf16[2912,364]{1,0:T(8,128)(2,1)} async-done(((bf16[728,364]{1,0:T(8,128)(2,1)}), bf16[2912,364]{1,0:T(8,128)(2,1)}) %all-gather.8.cloned.1.call-update) | async-done | bytes 2119952 | tf_op jit(solution)/shard_map/all_gather | solution.py:53
  139.3 5.4 %convolution_multiply_fusion.1 = f32[728,364]{1,0:T(8,128)S(1)} fusion(bf16[728,2912]{1,0:T(8,128)(2,1)} %get-tuple-element.6, bf16[2912,364]{1,0:T(8,128)(2,1)} %all-gather.8.cloned.1.call-done, f32[]{:T(128)S(6)} %mul.104), kind=kOutput, calls=%fused_computation.17 | convolution fusion | flops 1543578368 | bytes 7419780 | tf_op jit(solution)/shard_map/dot_general | solution.py:12
  144.7 1.5 fusion.17
  146.2 0.0 all-gather.10.cloned.1.call-update
  146.2 0.0 copy-start.1
  146.2 0.0 copy-start.2
  146.2 0.2 all-gather.12.cloned.1.call-start
  146.5 23.3 %all-gather.10.cloned.1.call-done = bf16[2912,364]{1,0:T(8,128)(2,1)} async-done(((bf16[728,364]{1,0:T(8,128)(2,1)}), bf16[2912,364]{1,0:T(8,128)(2,1)}) %all-gather.10.cloned.1.call-update) | async-done | bytes 2119952 | tf_op jit(solution)/shard_map/all_gather | solution.py:58
  169.7 6.2 %fusion.18 = bf16[728,364]{1,0:T(8,128)(2,1)} fusion(bf16[728,2912]{1,0:T(8,128)(2,1)} %get-tuple-element.6, bf16[2912,364]{1,0:T(8,128)(2,1)} %all-gather.10.cloned.1.call-done, f32[]{:T(128)S(6)} %rsqrt.3), kind=kOutput, calls=%fused_computation.27 | convolution fusion | flops 1543843328 | bytes 6889796 | tf_op jit(solution)/shard_map/dot_general | solution.py:12
  175.9 0.0 all-gather.12.cloned.1.call-update
  176.0 0.0 copy-done.1
  176.0 0.1 iota_subtract_fusion.1
  176.1 0.1 select_reduce_fusion
  176.2 0.0 copy-done.2
  176.2 2.5 %fusion.16 = f32[728,364]{1,0:T(8,128)S(1)} fusion(bf16[2912,364]{1,0:T(8,128)(2,1)S(1)} %copy-done.2, s32[728]{0:T(1024)S(1)} %iota_add_fusion, f32[]{:T(128)S(6)} %rsqrt.3), kind=kOutput, calls=%fused_computation.25 | convolution fusion | flops 1546493184 | bytes 3182820 | tf_op jit(solution)/shard_map/dot_general | solution.py:12
  178.7 0.0 copy-start
  178.7 20.7 %all-gather.12.cloned.1.call-done = bf16[2912,364]{1,0:T(8,128)(2,1)} async-done(((bf16[728,364]{1,0:T(8,128)(2,1)}), bf16[2912,364]{1,0:T(8,128)(2,1)}) %all-gather.12.cloned.1.call-update) | async-done | bytes 2119952 | tf_op jit(solution)/shard_map/all_gather | solution.py:59
  199.5 4.1 %fusion.13 = f32[728,364]{1,0:T(8,128)S(1)} fusion(f32[728,364]{1,0:T(8,128)S(1)} %fusion.16, bf16[2912,364]{1,0:T(8,128)(2,1)} %all-gather.12.cloned.1.call-done, s32[728]{0:T(1024)S(1)} %iota_add_fusion), kind=kOutput, calls=%fused_computation.22 | convolution fusion | flops 1545963264 | bytes 4242784 | tf_op jit(solution)/shard_map/dot_general | solution.py:12
  203.6 0.0 copy-done
  203.6 1.6 convolution_multiply_fusion.3
  (6 shorter events, 0.0 us)
Async XLA Ops:
  6.5 84.7 %all-gather.14.cloned.1.call-start = ((), (), s32[]{:S(2)}) async-start(), calls=%async_computation.3 | async-start | bytes 5031936 | tf_op jit(solution)/shard_map/all_gather | solution.py:28
  7.3 132.1 %all-gather.8.cloned.1.call-start = ((), (), s32[]{:S(2)}) async-start(), calls=%async_computation | async-start | bytes 2795520 | tf_op jit(solution)/shard_map/all_gather | solution.py:53
  117.1 52.6 %all-gather.10.cloned.1.call-start = ((), (), s32[]{:S(2)}) async-start(), calls=%async_computation.1 | async-start | bytes 2795520 | tf_op jit(solution)/shard_map/all_gather | solution.py:58
  146.2 29.8 %copy-start.1 = (s32[224]{0:T(256)S(1)}, s32[224]{0:T(256)}, u32[]{:S(2)}) copy-start(s32[224]{0:T(256)} %param.4) | copy-start | bytes 2692
  146.2 30.0 %copy-start.2 = (bf16[2912,364]{1,0:T(8,128)(2,1)S(1)}, bf16[2912,364]{1,0:T(8,128)(2,1)}, u32[]{:S(2)}) copy-start(bf16[2912,364]{1,0:T(8,128)(2,1)} %all-gather.8.cloned.1.call-done) | copy-start | bytes 6359812
  146.2 53.2 %all-gather.12.cloned.1.call-start = ((), (), s32[]{:S(2)}) async-start(), calls=%async_computation.2 | async-start | bytes 2795520 | tf_op jit(solution)/shard_map/all_gather | solution.py:59
  178.7 24.9 %copy-start = (s32[56,28]{0,1:T(8,128)S(1)}, s32[56,28]{0,1:T(8,128)}, u32[]{:S(2)}) copy-start(s32[56,28]{0,1:T(8,128)} %param.5) | copy-start | bytes 18820
Sparse Core Ops, SparseCore 0:
  9.5 81.6 all-gather.13
  117.2 22.0 all-gather.7
  146.3 23.3 all-gather.9
  176.1 23.3 all-gather.11

commit v2 on v1

v2 whole, which is shorter than its diff:
```python
import functools

import jax
import jax.numpy as jnp
from jax import lax
from jax.experimental import pallas as pl
from jax.experimental.pallas import tpu as pltpu
from jax.sharding import PartitionSpec as P

NBF = 13
LANE = 128
BF = jnp.bfloat16
F32 = jnp.float32
I32 = jnp.int32
MESH = pl.DeviceIdType.MESH


def up(n, k):
    return -(-n // k) * k


def mm(a, b):
    return jnp.dot(a, b, preferred_element_type=F32)


def mm_nt(a, b):
    return lax.dot_general(a, b, (((1,), (1,)), ((), ())), preferred_element_type=F32)


def spread(rows, lanes, base, count):
    i = lax.broadcasted_iota(I32, (rows, lanes), 0)
    a = lax.broadcasted_iota(I32, (rows, lanes), 1) - base
    hit = (a >= 0) & (a < count) & (i >= a * NBF) & (i < a * NBF + NBF)
    return jnp.where(hit, 1.0, 0.0).astype(BF)


def kernel(
    n_row, n_col, atoms_col, order,
    h_ref, pat_ref, selrow_ref, selcol_ref, poscol_ref, posrow_ref,
    out_ref,
    panel, m, bt, st, ct, acc, pt_in, pt_all, pt_old, tot, tot_all, er,
    own_sem, p1_send, p1_recv, p2_send, p2_recv, t_send, t_recv,
    g_send, g_recv, r_send, r_recv, f_send,
):
    ratio = n_col // n_row
    blk = h_ref.shape[2]
    live = up(atoms_col * NBF, 16)
    av = pat_ref.shape[0]
    outer = n_col // 2
    nx = n_row // 2
    pieces = blk // LANE
    row = lax.axis_index("row")
    col = lax.axis_index("col")
    hi, lo = col // 2, col % 2
    x, core = row // 2, row % 2
    peer_row = x * 2 + 1 - core

    def chunk_piece(c, t):
        return panel.at[c, t, pl.ds(0, live), :]

    own = []
    for t in range(ratio):
        cp = pltpu.make_async_copy(h_ref.at[t, pl.ds(0, live), :], chunk_piece(col, t), own_sem.at[t])
        cp.start()
        own.append(cp)

    barrier = pltpu.get_barrier_semaphore()
    for k in range(1, n_row):
        pl.semaphore_signal(barrier, inc=1, device_id={"row": (row + k) % n_row, "col": col}, device_id_type=MESH)
    for k in range(1, n_col):
        pl.semaphore_signal(barrier, inc=1, device_id={"row": row, "col": (col + k) % n_col}, device_id_type=MESH)
    pl.semaphore_wait(barrier, n_row + n_col - 2)

    def hop(c, t, way):
        to = [col + 2, col - 2, hi * 2 + 1 - lo][way]
        return pltpu.make_async_remote_copy(
            src_ref=chunk_piece(c, t), dst_ref=chunk_piece(c, t),
            send_sem=g_send.at[way, c, t], recv_sem=g_recv.at[c, t],
            device_id={"row": row, "col": to}, device_id_type=MESH,
        )

    for t in range(ratio):
        own[t].wait()

        @pl.when(hi + 1 < outer)
        def _():
            hop(col, t, 0).start()

        @pl.when(hi > 0)
        def _():
            hop(col, t, 1).start()

        hop(col, t, 2).start()

    def p1(k):
        return pltpu.make_async_remote_copy(
            src_ref=pat_ref, dst_ref=pt_in.at[row], send_sem=p1_send.at[k], recv_sem=p1_recv.at[row],
            device_id={"row": (row + k) % n_row, "col": col}, device_id_type=MESH,
        )

    def p2(k):
        return pltpu.make_async_remote_copy(
            src_ref=pt_all.at[col], dst_ref=pt_all.at[col], send_sem=p2_send.at[k], recv_sem=p2_recv.at[col],
            device_id={"row": row, "col": (col + k) % n_col}, device_id_type=MESH,
        )

    for k in range(1, n_row):
        p1(k).start()
    panel[:, :, live:, :] = jnp.zeros((n_col, ratio, blk - live, blk), BF)
    for t in range(ratio):
        er[t * blk : (t + 1) * blk, :] = spread(blk, LANE, t * atoms_col, atoms_col)
    ec = spread(blk, av, 0, atoms_col)
    pt_in[row] = pat_ref[...]
    acc[...] = jnp.zeros_like(acc)
    tot[...] = jnp.zeros_like(tot)
    for k in range(1, n_row):
        src = (row + k) % n_row
        pltpu.make_async_copy(pt_in.at[src], pt_in.at[src], p1_recv.at[src]).wait()
    old_rows = jnp.zeros((av, LANE), F32)
    for r in range(n_row):
        old_rows += mm(pt_in[r], selrow_ref[r])
    pt_all[col] = old_rows.astype(BF)
    for k in range(1, n_col):
        p2(k).start()
    for k in range(1, n_col):
        src = (col + k) % n_col
        pltpu.make_async_copy(pt_all.at[src], pt_all.at[src], p2_recv.at[src]).wait()
    everything = pt_all[...].reshape(n_col * av, LANE)
    for c in range(n_col):
        pt_old[c] = mm(selcol_ref[c], everything).astype(BF)

    def arrived(c, t):
        pltpu.make_async_copy(chunk_piece(c, t), chunk_piece(c, t), g_recv.at[c, t]).wait()

    def process(c):
        mask_rows = mm_nt(er[...], pt_old[c]).astype(BF)
        keep = mm_nt(mask_rows, ec)
        j = lax.broadcasted_iota(I32, (blk, blk), 1)
        pick = jnp.where(poscol_ref[...] == j + c * blk, 1.0, 0.0).astype(BF)
        for t in range(ratio):
            part = jnp.where(keep[t * blk : (t + 1) * blk] > 0.5, panel[c, t].astype(F32), 0.0)
            tot[...] += jnp.sum((part * part).reshape(blk // 8, 8, blk), axis=0)
            part = part.astype(BF)
            m[c, t * blk : (t + 1) * blk, :] = part
            acc[:, t * blk : (t + 1) * blk] += mm_nt(pick, part)

    def step(d, _):
        for way in range(2):
            src = hi - d if way == 0 else hi + d
            ok = (d > 0) & (d < outer) & (src >= 0) & (src < outer)

            @pl.when(ok)
            def _():
                c = src * 2 + lo
                more = hi + 1 < outer if way == 0 else hi > 0
                for t in range(ratio):
                    arrived(c, t)

                    @pl.when(more)
                    def _():
                        hop(c, t, way).start()

                    hop(c, t, 2).start()

        def candidate(k, _):
            kind, way = k // 2, k % 2
            dist = d - kind
            src = hi + (1 - 2 * way) * dist
            ok = (dist >= 0) & (dist < outer) & (src >= 0) & (src < outer) & ((dist > 0) | (way == 0))

            @pl.when(ok)
            def _():
                c = src * 2 + jnp.where(kind == 0, lo, 1 - lo)

                @pl.when(kind == 1)
                def _():
                    for t in range(ratio):
                        arrived(c, t)

                process(c)

            return 0

        lax.fori_loop(0, 4, candidate, 0)
        return 0

    lax.fori_loop(0, outer + 1, step, 0)

    def share(buf, stage, p):
        def part(r):
            return buf.at[r, pl.ds(p * LANE, LANE), :]

        def send(r, to, sem):
            return pltpu.make_async_remote_copy(
                src_ref=part(r), dst_ref=part(r), send_sem=sem, recv_sem=r_recv.at[stage, p, r],
                device_id={"row": to, "col": col}, device_id_type=MESH,
            )

        return (
            [send(row, (x + k) % nx * 2 + core, r_send.at[stage, p, k]) for k in range(1, nx)]
            + [send(row, peer_row, r_send.at[stage, p, 0])],
            [send((x + k) % nx * 2 + core, peer_row, f_send.at[stage, p, k]) for k in range(1, nx)],
        )

    def start_own(buf, stage, p):
        for cp in share(buf, stage, p)[0]:
            cp.start()

    def got(buf, stage, p, r):
        ref = buf.at[r, pl.ds(p * LANE, LANE), :]
        pltpu.make_async_copy(ref, ref, r_recv.at[stage, p, r]).wait()

    def relay(buf, stage, p):
        onward = share(buf, stage, p)[1]
        for k in range(1, nx):
            got(buf, stage, p, (x + k) % nx * 2 + core)
            onward[k - 1].start()

    def finish(buf, stage, p):
        for k in range(nx):
            got(buf, stage, p, (x + k) % nx * 2 + 1 - core)

    def drain(buf, stage, p):
        first, onward = share(buf, stage, p)
        for cp in first + onward:
            cp.wait_send()

    def t_copy(k):
        return pltpu.make_async_remote_copy(
            src_ref=tot_all.at[row], dst_ref=tot_all.at[row], send_sem=t_send.at[k], recv_sem=t_recv.at[row],
            device_id={"row": (row + k) % n_row, "col": col}, device_id_type=MESH,
        )

    part_sum = tot[:, 0:LANE]
    for q in range(1, pieces):
        part_sum += tot[:, q * LANE : (q + 1) * LANE]
    tot_all[row] = part_sum
    for p in range(pieces):
        bt[row, p * LANE : (p + 1) * LANE, :] = acc[p * LANE : (p + 1) * LANE, :].astype(BF)
        start_own(bt, 0, p)
    for k in range(1, n_row):
        t_copy(k).start()
    for k in range(1, n_row):
        src = (row + k) % n_row
        pltpu.make_async_copy(tot_all.at[src], tot_all.at[src], t_recv.at[src]).wait()
    total = jnp.sum(jnp.sum(tot_all[...], axis=0), axis=(0, 1), keepdims=True)
    s = lax.rsqrt(total / order)

    def panel_product(buf, p):
        result = jnp.zeros((LANE, ratio * blk), F32)
        for c in range(n_col):
            t = c % ratio
            result += mm_nt(buf[c // ratio, p * LANE : (p + 1) * LANE, t * blk : (t + 1) * blk], m[c])
        return result

    mask_cols = mm(ec, pt_all[col]).astype(BF)
    for p in range(pieces):
        relay(bt, 0, p)
    for p in range(pieces):
        finish(bt, 0, p)
        keep = mm_nt(mask_cols[p * LANE : (p + 1) * LANE], er[...])
        square = panel_product(bt, p) * (s * s)
        st[row, p * LANE : (p + 1) * LANE, :] = jnp.where(keep > 0.5, square, 0.0).astype(BF)
        start_own(st, 1, p)

    def pick_rows(r):
        j = lax.broadcasted_iota(I32, (ratio * blk, ratio * blk), 1)
        return jnp.where(posrow_ref[...] == j + r * (ratio * blk), 1.0, 0.0).astype(BF)

    start = jnp.zeros((ratio * blk, blk), F32)
    for r in range(n_row):
        start += mm_nt(pick_rows(r), bt[r])
    start = 1.5 * (start * s).astype(BF).astype(F32)
    for t in range(ratio):
        out_ref[t] = start[t * blk : (t + 1) * blk]
    for p in range(pieces):
        relay(st, 1, p)
        finish(st, 1, p)
        cube = panel_product(st, p) * s
        ct[row, p * LANE : (p + 1) * LANE, :] = cube.astype(BF)
        start_own(ct, 2, p)
    for p in range(pieces):
        relay(ct, 2, p)
    for p in range(pieces):
        finish(ct, 2, p)
    mine = mm_nt(er[...], pat_ref[...]).astype(BF)
    keep = mm_nt(mine, ec)
    cube = jnp.zeros((ratio * blk, blk), F32)
    for r in range(n_row):
        cube += mm_nt(pick_rows(r), ct[r])
    for t in range(ratio):
        part = slice(t * blk, (t + 1) * blk)
        out_ref[t] = jnp.where(keep[part] > 0.5, out_ref[t] - 0.5 * cube[part], 0.0)

    for k in range(1, n_row):
        p1(k).wait_send()
        t_copy(k).wait_send()
    for k in range(1, n_col):
        p2(k).wait_send()

    def sent(q, _):
        c = q * 2 + lo
        for t in range(ratio):

            @pl.when((q <= hi) & (hi + 1 < outer))
            def _():
                hop(c, t, 0).wait_send()

            @pl.when((q >= hi) & (hi > 0))
            def _():
                hop(c, t, 1).wait_send()

            hop(c, t, 2).wait_send()
        return 0

    lax.fori_loop(0, outer, sent, 0)
    for stage, buf in enumerate((bt, st, ct)):
        for p in range(pieces):
            drain(buf, stage, p)


def on_device(hamiltonian, new_atom, pattern):
    rows_here, cols_here = hamiltonian.shape
    n_row, n_col = lax.axis_size("row"), lax.axis_size("col")
    ratio = n_col // n_row
    ar, ac = pattern.shape
    order = rows_here * n_row
    blk = up(cols_here, LANE)
    av = up(ac, 16)
    row_here = lax.axis_index("row")
    col_here = lax.axis_index("col")
    pad = blk - cols_here
    h = jnp.pad(hamiltonian.reshape(ratio, cols_here, cols_here), ((0, 0), (0, pad), (0, pad)))
    pat_t = jnp.pad(pattern.astype(BF).T, ((0, av - ac), (0, LANE - ar)))
    by_row = jnp.pad(new_atom.reshape(n_row, ar), ((0, 0), (0, LANE - ar)), constant_values=-1)
    i = jnp.arange(LANE, dtype=I32)
    selrow = ((by_row[:, :, None] == row_here * ar + i) & (i < ar)).astype(BF)
    by_col = jnp.pad(new_atom.reshape(n_col, ac), ((0, 0), (0, av - ac)), constant_values=-1).reshape(-1)
    v = jnp.arange(av, dtype=I32)
    old = jnp.arange(n_col, dtype=I32)[:, None] * ac + v[None, :]
    selcol = ((by_col[None, None, :] == old[:, :, None]) & (v < ac)[None, :, None]).astype(BF)
    place = new_atom // ac * blk + new_atom % ac * NBF

    def positions(here):
        mine = lax.dynamic_slice_in_dim(place, here * ac, ac)
        q = jnp.arange(blk, dtype=I32)
        a = jnp.arange(ac, dtype=I32)
        hit = (q[:, None] >= a * NBF) & (q[:, None] < a * NBF + NBF)
        base = jnp.sum(jnp.where(hit, (mine - a * NBF)[None, :], 0), axis=1)
        return jnp.where(q < ac * NBF, base + q, -1)

    poscol = positions(col_here)[:, None]
    posrow = jnp.concatenate([positions(row_here * ratio + t) for t in range(ratio)])[:, None]
    pieces = blk // LANE
    vm = pl.BlockSpec(memory_space=pltpu.VMEM)
    dma = pltpu.SemaphoreType.DMA
    wide = ratio * blk
    out = pl.pallas_call(
        functools.partial(kernel, n_row, n_col, ac, float(order)),
        out_shape=jax.ShapeDtypeStruct((ratio, blk, blk), F32),
        in_specs=[pl.BlockSpec(memory_space=pl.ANY)] + [vm] * 5,
        out_specs=vm,
        scratch_shapes=[
            pltpu.VMEM((n_col, ratio, blk, blk), BF),
            pltpu.VMEM((n_col, wide, blk), BF),
            pltpu.VMEM((n_row, blk, wide), BF),
            pltpu.VMEM((n_row, blk, wide), BF),
            pltpu.VMEM((n_row, blk, wide), BF),
            pltpu.VMEM((blk, wide), F32),
            pltpu.VMEM((n_row, av, LANE), BF),
            pltpu.VMEM((n_col, av, LANE), BF),
            pltpu.VMEM((n_col, av, LANE), BF),
            pltpu.VMEM((8, blk), F32),
            pltpu.VMEM((n_row, 8, LANE), F32),
            pltpu.VMEM((wide, LANE), BF),
            dma((ratio,)),
            dma((n_row,)),
            dma((n_row,)),
            dma((n_col,)),
            dma((n_col,)),
            dma((n_row,)),
            dma((n_row,)),
            dma((3, n_col, ratio)),
            dma((n_col, ratio)),
            dma((3, pieces, n_row)),
            dma((3, pieces, n_row)),
            dma((3, pieces, n_row)),
        ],
        compiler_params=pltpu.CompilerParams(
            collective_id=0, has_side_effects=True, vmem_limit_bytes=60 * 1024 * 1024
        ),
    )(h, pat_t, selrow, selcol, poscol, posrow)
    return out[:, :cols_here, :cols_here].reshape(rows_here, cols_here)


def solution(mesh):
    in_specs = (P("row", "col"), P(), P("row", "col"))
    out_specs = P("row", "col")
    return jax.shard_map(
        on_device, mesh=mesh, in_specs=in_specs, out_specs=out_specs, check_vma=False
    )
```

time: 212 us -> 126 us (0.59)
  Pallas kernels: 0 us -> 114 us
  blocking collectives: 81.4 us -> 0 us
  waiting for transfers between devices: 64.9 us -> 0 us
  matrix products: 35.5 us -> 0 us
  between operations: 14 us -> 0.07 us
  local copies, waits for them, and re-layouts: 13.8 us -> 6.58 us
  other arithmetic: 1.79 us -> 4.13 us
    pallas_call x0 -> x1, Pallas kernels: none -> 114 us  [on_device(): pl.pallas_call(functools.partial(kernel, n_row, n_col, ac, float(order)),...]
    all_gather x1 -> x0, blocking collectives: 75.1 us -> none  [on_device(): lax.all_gather(pattern.astype(BF), ('row', 'col'), axis=0, tiled=False)]
    all_gather x4 -> x0, waiting for transfers between devices: 64.2 us -> none  [the longest x1 23.3 us: on_device(): square = lax.all_gather(square, 'row', axis=0, tiled=True)]
    dot_general x10 -> x0, matrix products: 35.5 us -> none  [mm(): return jnp.dot(a, b, preferred_element_type=F32)]
    unnamed x7 -> x2, local copies, waits for them, and re-layouts: 8.62 us -> 0.01 us
    psum x1 -> x0, blocking collectives: 6.25 us -> none  [on_device(): total = lax.psum(jnp.sum(m.astype(F32) ** 2), 'row')]
    all_gather x1 -> x0, local copies, waits for them, and re-layouts: 4.87 us -> none  [on_device(): panel = lax.all_gather(hamiltonian, 'col', axis=1, tiled=True)]
    reshape x2 -> x4, local copies, waits for them, and re-layouts: 0.35 us -> 2.73 us  [the longest x1 1.1 us: on_device(): return out[:, :cols_here, :cols_here].reshape(rows_here, cols_here)]
  transfers between devices with their start and end apart: 4 -> 0, of which waited for: 4 -> 0; matrix products, arithmetic and copies ran while one was open for 3% -> 0% of each run, Pallas kernels for 0% -> 0%
where the time goes in v2:
time: 126 us; the launch traced here: 125 us
  Pallas kernels  114 us (90%)
  local copies, waits for them, and re-layouts  6.58 us (5%)
  other arithmetic  4.13 us (3%)
    pallas_call x1, Pallas kernels, on_device(): pl.pallas_call(functools.partial(kernel, n_row, n_col, ac, float(order)),...  114 us

profile of v2, /device:TPU:0, one launch (start us, length us, event | category | flops | bytes accessed | tf_op | source)
XLA Modules:
  0.0 125.1 jit_solution(8737875435198156660)
XLA Ops:
  0.0 0.0 copy-start
  0.0 0.7 fusion.3
  0.8 0.1 dynamic-slice_subtract_fusion.2
  0.9 0.8 reshape.82
  1.7 0.1 iota_add_fusion
  1.7 0.1 select_reduce_fusion.1
  1.9 0.8 reshape.83
  2.6 0.1 eq.33
  2.7 0.7 convert_bitcast_fusion
  3.4 0.6 pad.17.pat_ref
  4.0 0.8 and_convert_fusion.selcol_ref
  4.8 0.8 and_convert_fusion.1.selrow_ref
  5.6 0.8 fusion.poscol_ref
  6.4 0.9 broadcast_in_dim.65.posrow_ref
  7.3 0.0 copy-done
  7.3 0.1 reshape.81
  7.4 0.9 pad.16.h_ref
  8.3 114.3 %shard_map.37 = f32[2,384,384]{2,1,0:T(8,128)} custom-call(bf16[2,384,384]{2,1,0:T(8,128)(2,1)} %pad.16.h_ref, bf16[32,128]{1,0:T(8,128)(2,1)} %pad.17.pat_ref, bf16[4,128,128]{2,1,0:T(8,128)(2,1)} %and_convert_fusion.1.selrow_ref, bf16[8,32,256]{2,1,0:T(8,128)(2,1)} %and_convert_fusion.selcol_ref, s32[384,1]{1,0:T(8,128)} %fusion.poscol_ref, ...), custom_call_target="tpu_custom_call" | custom-call | tf_op jit(solution)/shard_map/pallas_call | solution.py:358
  122.7 1.3 %slice.3 = f32[2,364,364]{2,1,0:T(8,128)S(1)} slice(f32[2,384,384]{2,1,0:T(8,128)} %shard_map.37), slice={[0:2], [0:364], [0:364]} | slice | bytes 2119936 | tf_op jit(solution)/shard_map/slice | solution.py:393
  124.0 1.1 reshape.84
  (10 shorter events, 0.1 us)
Async XLA Ops:
  0.0 7.3 %copy-start = (bf16[728,364]{1,0:T(8,128)(2,1)S(1)}, bf16[728,364]{1,0:T(8,128)(2,1)}, u32[]{:S(2)}) copy-start(bf16[728,364]{1,0:T(8,128)(2,1)} %param.3) | copy-start | bytes 1589956
